TPU v7x, 32 devices: a whole 2x2x4 slice. The times are simulated.
32 devices in a mesh: level: 4 (over z), dev: 8 (over y, x, core).
Axes of the slice: x: 2, y: 2, z: 4, core: 2. Of those that a mesh axis runs over, the one named last changes fastest.
Arguments:
- fields: float32 [4, 128, 12, 128], P('level', 'dev'), may hold values from -6 to 6
- own_src: int32 [4, 128], P('level', 'dev'), may hold values from 0 to 15
- own_weight: bfloat16 [4, 128, 128, 128], P('level', 'dev'), may hold values from 0 to 1, as said below
- send_block: int32 [4, 8, 8, 2], P('level', 'dev'), may hold values from 0 to 15
- send_target: int32 [4, 8, 8, 2], P('level', 'dev'), may hold values from 0 to 15
- send_count: int32 [4, 8, 8], P('level', 'dev'), may hold values from 0 to 2, as said below
- send_weight: bfloat16 [4, 8, 8, 2, 128, 128], P('level', 'dev'), may hold values from 0 to 1, as said below
- left_block: int32 [4, 8, 4, 2], P('level', 'dev'), may hold values from 0 to 15
- left_target: int32 [4, 8, 4, 2], P('level', 'dev'), may hold values from 0 to 15
- left_count: int32 [4, 8, 4], P('level', 'dev'), may hold values from 0 to 2, as said below
- left_weight: bfloat16 [4, 8, 4, 2, 128, 128], P('level', 'dev'), may hold values from 0 to 1, as said below
Outputs:
- remapped: float32 [4, 128, 12, 128], P('level', 'dev')
- totals: float32 [12], replicated
Inputs may be any that keep to these rules, and one draw needn't show every extreme that they name: send_count[l, s, s] = 0; for every level some receiver device gets 2 live slots from every other device of the level. left_count[m, q, m] = 0; for every device index some receiver level gets 2 live slots from every other level. `own_weight`: nonnegative; entry [k, i] is zero where old cell k and new cell i differ by more than 3; each column sums to a positive intersect fraction of at most 1. `send_weight`: nonnegative; entry [k, i] is zero where old cell k and new cell i differ by more than 3; each column sums to a positive intersect fraction of at most 1. `left_weight`: nonnegative; entry [k, i] is zero where old cell k and new cell i differ by more than 3; each column sums to a positive intersect fraction of at most 1.
All inputs are finite; a program needn't handle non-finite values.
Results may differ from a plain program's by a relative error of at most 0.0045.
Values may be sent and summed in bfloat16 or wider, within the bound.
A program may use at most 64 MiB of HBM per device.

v0:
```python
import jax
import jax.numpy as jnp
from jax import lax
from jax.sharding import PartitionSpec as P


def pick_donors(rounded, block_index, count):
    donors = rounded[block_index]
    slots = block_index.shape[1]
    valid = lax.broadcasted_iota(jnp.int32, (1, slots), 1) < count[:, None]
    return jnp.where(valid[:, :, None, None], donors, jnp.zeros_like(donors))


def apply_weights(donors, weights):
    return jnp.einsum("pcmk,pcki->pcmi", donors, weights, preferred_element_type=jnp.float32)


def place_terms(contrib, target, blocks):
    comp = contrib.shape[2]
    cells = contrib.shape[3]
    flat_target = target.reshape(-1)
    onehot = (flat_target[:, None] == lax.broadcasted_iota(jnp.int32, (1, blocks), 1)).astype(
        jnp.float32
    )
    return jnp.einsum(
        "sb,smi->bmi", onehot, contrib.reshape(-1, comp, cells), precision=lax.Precision.HIGHEST
    )


def body(
    fields,
    own_src,
    own_weight,
    send_block,
    send_target,
    send_count,
    send_weight,
    left_block,
    left_target,
    left_count,
    left_weight,
):
    local = fields[0]
    blocks = local.shape[0]
    rounded = local.astype(jnp.bfloat16)
    own = jnp.einsum(
        "bmk,bki->bmi", rounded[own_src[0]], own_weight[0], preferred_element_type=jnp.float32
    )
    donors = pick_donors(rounded, send_block[0, 0], send_count[0, 0])
    strays = pick_donors(rounded, left_block[0, 0], left_count[0, 0])
    intra_terms, intra_target = (
        lax.all_to_all(
            apply_weights(donors, send_weight[0, 0]), "dev", split_axis=0, concat_axis=0, tiled=True
        ),
        lax.all_to_all(send_target[0, 0], "dev", split_axis=0, concat_axis=0, tiled=True),
    )
    left_terms, left_where = (
        lax.all_to_all(
            apply_weights(strays, left_weight[0, 0]),
            "level",
            split_axis=0,
            concat_axis=0,
            tiled=True,
        ),
        lax.all_to_all(left_target[0, 0], "level", split_axis=0, concat_axis=0, tiled=True),
    )
    remapped = (
        own
        + place_terms(intra_terms, intra_target, blocks)
        + place_terms(left_terms, left_where, blocks)
    )
    sums = lax.psum(jnp.sum(remapped, axis=(0, 2)), ("level", "dev"))
    totals = sums / (remapped.shape[2] * blocks)
    return (remapped[None], totals)


def solution(mesh):
    in_specs = (
        P("level", "dev", None, None),
        P("level", "dev"),
        P("level", "dev", None, None),
        P("level", "dev", None, None),
        P("level", "dev", None, None),
        P("level", "dev", None),
        P("level", "dev", None, None, None, None),
        P("level", "dev", None, None),
        P("level", "dev", None, None),
        P("level", "dev", None),
        P("level", "dev", None, None, None, None),
    )
    out_specs = (P("level", "dev", None, None), P())
    return jax.shard_map(body, mesh=mesh, in_specs=in_specs, out_specs=out_specs, check_vma=False)
```

profile of v0, /device:TPU:0, one launch (start us, length us, event | category | flops | bytes accessed | tf_op | source)
XLA Modules:
  0.0 84.1 jit_solution(18198775144529475194)
XLA Ops:
  0.6 0.0 copy-start
  0.6 0.0 copy-start.3
  0.7 0.0 copy-start.2
  0.7 0.0 copy-start.1
  0.7 0.7 copy-done.3
  1.4 0.6 copy.41
  2.0 6.3 %all-to-all-start.2 = ((s32[4,1,2]{2,1,0:T(1,128)}), s32[4,1,2]{2,1,0:T(1,128)S(1)}, u32[]{:S(2)}, u32[]{:S(2)}) async-start(s32[4,1,2]{2,1,0:T(1,128)} %copy.41), calls=%async_computation.2 | async-start | bytes 4096 | tf_op jit(solution)/shard_map/all_to_all | solution.py:65
  8.4 0.7 fusion.21
  9.0 0.7 iota_compare_fusion.3
  9.8 0.7 compare_select_fusion.1
  10.4 0.7 iota_compare_fusion.2
  11.2 0.7 compare_select_fusion
  11.9 0.1 copy.42
  11.9 0.1 reshape.173
  12.0 0.1 copy.37
  12.1 0.1 reshape.165
  12.2 1.3 %copy.36 = s32[8,1,2]{2,1,0:T(1,128)} copy(s32[8,1,2]{0,2,1:T(2,128)} %bitcast.53) | data formatting | bytes 128 | tf_op jit(solution)/shard_map/all_to_all | solution.py:55
  13.6 0.9 %copy.52 = bf16[1,16,12,128]{3,2,1,0:T(8,128)(2,1)S(1)} copy(f32[1,16,12,128]{3,1,2,0:T(8,128)} %param.11) | data formatting | bytes 147456 | tf_op args[0]
  14.5 0.6 gather_fusion.2
  15.1 0.6 gather_fusion.1
  15.6 0.0 copy-done.2
  15.6 0.2 fusion.4
  15.9 0.0 copy-done.1
  15.9 0.3 fusion.1
  16.2 0.0 all-to-all-done.2
  16.2 3.7 %all-to-all-start = ((s32[8,1,2]{2,1,0:T(1,128)}), s32[8,1,2]{2,1,0:T(1,128)S(1)}, u32[]{:S(2)}, u32[]{:S(2)}) async-start(s32[8,1,2]{2,1,0:T(1,128)} %copy.36), calls=%async_computation | async-start | bytes 8192 | tf_op jit(solution)/shard_map/all_to_all | solution.py:55
  19.9 0.6 copy.43
  20.6 4.0 %all-to-all-done = s32[8,1,2]{2,1,0:T(1,128)S(1)} async-done(((s32[8,1,2]{2,1,0:T(1,128)}), s32[8,1,2]{2,1,0:T(1,128)S(1)}, u32[]{:S(2)}, u32[]{:S(2)}) %all-to-all-start) | async-done | bytes 96 | tf_op jit(solution)/shard_map/all_to_all | solution.py:55
  24.5 5.1 %all-to-all-start.3 = ((f32[4,2,12,128]{3,1,2,0:T(2,128)}), f32[4,2,12,128]{3,1,2,0:T(2,128)S(1)}, u32[]{:S(2)}, u32[]{:S(2)}) async-start(f32[4,2,12,128]{3,1,2,0:T(2,128)} %copy.43), calls=%async_computation.3 | async-start | bytes 98304 | tf_op jit(solution)/shard_map/all_to_all | solution.py:58
  29.6 0.6 gather_fusion
  30.2 0.7 copy.38
  30.9 0.5 broadcast.122
  31.4 0.7 reduce.6
  32.1 0.1 eq.34
  32.2 0.7 reduce.7
  32.8 0.1 eq.30
  32.9 2.4 %all-to-all-done.3 = f32[4,2,12,128]{3,1,2,0:T(2,128)S(1)} async-done(((f32[4,2,12,128]{3,1,2,0:T(2,128)}), f32[4,2,12,128]{3,1,2,0:T(2,128)S(1)}, u32[]{:S(2)}, u32[]{:S(2)}) %all-to-all-start.3) | async-done | bytes 49184 | tf_op jit(solution)/shard_map/all_to_all | solution.py:58
  35.3 3.4 %all-to-all-start.1 = ((f32[8,2,12,128]{3,1,2,0:T(2,128)}), f32[8,2,12,128]{3,1,2,0:T(2,128)S(1)}, u32[]{:S(2)}, u32[]{:S(2)}) async-start(f32[8,2,12,128]{3,1,2,0:T(2,128)} %copy.38), calls=%async_computation.1 | async-start | bytes 196608 | tf_op jit(solution)/shard_map/all_to_all | solution.py:52
  38.7 0.3 fusion.18
  39.0 4.8 %all-to-all-done.1 = f32[8,2,12,128]{3,1,2,0:T(2,128)S(1)} async-done(((f32[8,2,12,128]{3,1,2,0:T(2,128)}), f32[8,2,12,128]{3,1,2,0:T(2,128)S(1)}, u32[]{:S(2)}, u32[]{:S(2)}) %all-to-all-start.1) | async-done | bytes 98336 | tf_op jit(solution)/shard_map/all_to_all | solution.py:52
  43.9 0.2 fusion.14
  44.1 0.0 copy-done
  44.1 0.4 fusion.24
  44.4 38.5 %psum.7 = f32[12]{0:T(128)S(1)} all-reduce(f32[12]{0:T(128)S(1)} %get-tuple-element.8), channel_id=1, replica_groups=mesh['level'=4,'dev'=8] {'level','dev'}, use_global_device_ids=true, to_apply=%region_1.2 | all-reduce | flops 12 | bytes 96 | tf_op jit(solution)/shard_map/psum | solution.py:72
  82.9 0.5 broadcast_multiply_fusion
  83.4 0.7 copy.46
  (5 shorter events, 0.1 us)
Async XLA Ops:
  0.6 43.4 %copy-start = (bf16[1,16,128,128]{3,2,1,0:T(8,128)(2,1)S(1)}, bf16[1,16,128,128]{3,2,1,0:T(8,128)(2,1)}, u32[]{:S(2)}) copy-start(bf16[1,16,128,128]{3,2,1,0:T(8,128)(2,1)} %param.13) | copy-start | bytes 1572868
  0.6 0.7 copy-start.3
  0.7 15.0 %copy-start.2 = (bf16[1,1,4,2,128,128]{5,4,3,2,1,0:T(8,128)(2,1)S(1)}, bf16[1,1,4,2,128,128]{5,4,3,2,1,0:T(8,128)(2,1)}, u32[]{:S(2)}) copy-start(bf16[1,1,4,2,128,128]{5,4,3,2,1,0:T(8,128)(2,1)} %param.21) | copy-start | bytes 786436
  0.7 15.2 %copy-start.1 = (bf16[1,1,8,2,128,128]{5,4,3,2,1,0:T(8,128)(2,1)S(1)}, bf16[1,1,8,2,128,128]{5,4,3,2,1,0:T(8,128)(2,1)}, u32[]{:S(2)}) copy-start(bf16[1,1,8,2,128,128]{5,4,3,2,1,0:T(8,128)(2,1)} %param.17) | copy-start | bytes 1572868
  2.0 14.2 %all-to-all-start.2 = ((s32[4,1,2]{2,1,0:T(1,128)}), s32[4,1,2]{2,1,0:T(1,128)S(1)}, u32[]{:S(2)}, u32[]{:S(2)}) async-start(s32[4,1,2]{2,1,0:T(1,128)} %copy.41), calls=%async_computation.2 | async-start | bytes 4096 | tf_op jit(solution)/shard_map/all_to_all | solution.py:65
  16.2 8.3 %all-to-all-start = ((s32[8,1,2]{2,1,0:T(1,128)}), s32[8,1,2]{2,1,0:T(1,128)S(1)}, u32[]{:S(2)}, u32[]{:S(2)}) async-start(s32[8,1,2]{2,1,0:T(1,128)} %copy.36), calls=%async_computation | async-start | bytes 8192 | tf_op jit(solution)/shard_map/all_to_all | solution.py:55
  24.5 10.8 %all-to-all-start.3 = ((f32[4,2,12,128]{3,1,2,0:T(2,128)}), f32[4,2,12,128]{3,1,2,0:T(2,128)S(1)}, u32[]{:S(2)}, u32[]{:S(2)}) async-start(f32[4,2,12,128]{3,1,2,0:T(2,128)} %copy.43), calls=%async_computation.3 | async-start | bytes 98304 | tf_op jit(solution)/shard_map/all_to_all | solution.py:58
  35.3 8.5 %all-to-all-start.1 = ((f32[8,2,12,128]{3,1,2,0:T(2,128)}), f32[8,2,12,128]{3,1,2,0:T(2,128)S(1)}, u32[]{:S(2)}, u32[]{:S(2)}) async-start(f32[8,2,12,128]{3,1,2,0:T(2,128)} %copy.38), calls=%async_computation.1 | async-start | bytes 196608 | tf_op jit(solution)/shard_map/all_to_all | solution.py:52
where the time goes:
time: 84.7 us; the launch traced here: 84.1 us
  blocking collectives  38.5 us (45%)
  starting transfers between devices  18.5 us (22%)
  waiting for transfers between devices  11.2 us (13%)
  local copies, waits for them, and re-layouts  8.43 us (10%)
  other arithmetic  5.33 us (6%)
  matrix products  1.38 us (2%)
    psum x1, blocking collectives, body(): sums = lax.psum(jnp.sum(remapped, axis=(0, 2)), ('level', 'dev'))  38.5 us
    all_to_all x1, starting transfers between devices, body(): lax.all_to_all(left_target[0, 0], 'level', split_axis=0, concat_axis=0, t...  6.35 us
    all_to_all x1, starting transfers between devices, body(): lax.all_to_all(apply_weights(strays, left_weight[0, 0]), 'level', split_a...  5.09 us
    all_to_all x1, waiting for transfers between devices, body(): lax.all_to_all(apply_weights(donors, send_weight[0, 0]), 'dev', split_axi...  4.79 us
    all_to_all x1, waiting for transfers between devices, body(): lax.all_to_all(send_target[0, 0], 'dev', split_axis=0, concat_axis=0, til...  3.97 us
    all_to_all x1, starting transfers between devices, body(): lax.all_to_all(send_target[0, 0], 'dev', split_axis=0, concat_axis=0, til...  3.74 us
    all_to_all x1, starting transfers between devices, body(): lax.all_to_all(apply_weights(donors, send_weight[0, 0]), 'dev', split_axi...  3.36 us
    all_to_all x1, waiting for transfers between devices, body(): lax.all_to_all(apply_weights(strays, left_weight[0, 0]), 'level', split_a...  2.42 us
  transfers between devices with their start and end apart: 4, of which 3 were waited for; matrix products, arithmetic and copies ran while one was open for 14% of the time, Pallas kernels for 0%

commit v1 on v0

--- a/solution.py
+++ b/solution.py
@@ -69,7 +69,7 @@
         + place_terms(intra_terms, intra_target, blocks)
         + place_terms(left_terms, left_where, blocks)
     )
-    sums = lax.psum(jnp.sum(remapped, axis=(0, 2)), ("level", "dev"))
+    sums = lax.psum(lax.psum(jnp.sum(remapped, axis=(0, 2)), "dev"), "level")
     totals = sums / (remapped.shape[2] * blocks)
     return (remapped[None], totals)
 

time: 84.7 us -> 67.8 us (0.80)
  blocking collectives: 38.5 us -> 21.6 us
    psum x1 -> x2, blocking collectives: 38.5 us -> 21.6 us  [body(): sums = lax.psum(lax.psum(jnp.sum(remapped, axis=(0, 2)), 'dev'), 'level')]
  transfers between devices with their start and end apart: 4 -> 4, of which waited for: 3 -> 3; matrix products, arithmetic and copies ran while one was open for 14% -> 18% of each run, Pallas kernels for 0% -> 0%
where the time goes in v1:
time: 67.8 us; the launch traced here: 67.2 us
  blocking collectives  21.6 us (32%)
  starting transfers between devices  18.5 us (27%)
  waiting for transfers between devices  11.2 us (17%)
  local copies, waits for them, and re-layouts  8.47 us (12%)
  other arithmetic  5.33 us (8%)
  matrix products  1.37 us (2%)
  between operations  0.76 us (1%)
    psum x2, blocking collectives, body(): sums = lax.psum(lax.psum(jnp.sum(remapped, axis=(0, 2)), 'dev'), 'level')  21.6 us
    all_to_all x1, starting transfers between devices, body(): lax.all_to_all(left_target[0, 0], 'level', split_axis=0, concat_axis=0, t...  6.35 us
    all_to_all x1, starting transfers between devices, body(): lax.all_to_all(apply_weights(strays, left_weight[0, 0]), 'level', split_a...  5.09 us
    all_to_all x1, waiting for transfers between devices, body(): lax.all_to_all(apply_weights(donors, send_weight[0, 0]), 'dev', split_axi...  4.79 us
    all_to_all x1, waiting for transfers between devices, body(): lax.all_to_all(send_target[0, 0], 'dev', split_axis=0, concat_axis=0, til...  3.97 us
    all_to_all x1, starting transfers between devices, body(): lax.all_to_all(send_target[0, 0], 'dev', split_axis=0, concat_axis=0, til...  3.74 us
    all_to_all x1, starting transfers between devices, body(): lax.all_to_all(apply_weights(donors, send_weight[0, 0]), 'dev', split_axi...  3.36 us
    all_to_all x1, waiting for transfers between devices, body(): lax.all_to_all(apply_weights(strays, left_weight[0, 0]), 'level', split_a...  2.42 us
  transfers between devices with their start and end apart: 4, of which 3 were waited for; matrix products, arithmetic and copies ran while one was open for 18% of the time, Pallas kernels for 0%

profile of v1, /device:TPU:0, one launch (start us, length us, event | category | flops | bytes accessed | tf_op | source)
XLA Modules:
  0.0 67.2 jit_solution(16323190166845679909)
XLA Ops:
  0.6 0.0 copy-start
  0.6 0.0 copy-start.3
  0.7 0.0 copy-start.2
  0.7 0.0 copy-start.1
  0.7 0.7 %copy-done.3 = s32[1,1,4,2]{2,3,1,0:T(2,128)S(1)} copy-done((s32[1,1,4,2]{2,3,1,0:T(2,128)S(1)}, s32[1,1,4,2]{2,3,1,0:T(2,128)}, u32[]{:S(2)}) %copy-start.3) | copy-done | bytes 56
  1.4 0.7 %copy.41 = s32[4,1,2]{2,1,0:T(1,128)} copy(s32[4,1,2]{0,2,1:T(2,128)S(1)} %bitcast.52) | data formatting | bytes 64 | tf_op jit(solution)/shard_map/all_to_all | solution.py:65
  2.1 6.3 %all-to-all-start.2 = ((s32[4,1,2]{2,1,0:T(1,128)}), s32[4,1,2]{2,1,0:T(1,128)S(1)}, u32[]{:S(2)}, u32[]{:S(2)}) async-start(s32[4,1,2]{2,1,0:T(1,128)} %copy.41), calls=%async_computation.2 | async-start | bytes 4096 | tf_op jit(solution)/shard_map/all_to_all | solution.py:65
  8.4 0.7 fusion.21
  9.1 0.7 %iota_compare_fusion.3 = pred[4,2]{1,0:T(4,128)(4,1)S(1)} fusion(s32[4]{0:T(128)} %bitcast.54), kind=kLoop, calls=%fused_computation.32 | loop fusion | flops 8 | bytes 24 | tf_op jit(solution)/shard_map/lt | solution.py:10
  9.8 0.7 %compare_select_fusion.1 = s32[8,2,1]{0,1,2:T(2,128)S(1)} fusion(s32[1,1,8,2]{2,3,1,0:T(2,128)} %param.14), kind=kLoop, calls=%fused_computation.30 | loop fusion | flops 48 | bytes 128 | tf_op jit(solution)/shard_map/select_n | solution.py:8
  10.5 0.7 %iota_compare_fusion.2 = pred[8,2]{1,0:T(8,128)(4,1)S(1)} fusion(s32[8]{0:T(128)} %bitcast.55), kind=kLoop, calls=%fused_computation.25 | loop fusion | flops 16 | bytes 48 | tf_op jit(solution)/shard_map/lt | solution.py:10
  11.2 0.7 %compare_select_fusion = s32[4,2,1]{0,1,2:T(2,128)S(1)} fusion(s32[1,1,4,2]{2,3,1,0:T(2,128)} %param.18), kind=kLoop, calls=%fused_computation.29 | loop fusion | flops 24 | bytes 64 | tf_op jit(solution)/shard_map/select_n | solution.py:8
  11.9 0.1 copy.42
  12.0 0.1 reshape.173
  12.1 0.1 copy.37
  12.1 0.1 reshape.165
  12.2 1.3 %copy.36 = s32[8,1,2]{2,1,0:T(1,128)} copy(s32[8,1,2]{0,2,1:T(2,128)} %bitcast.53) | data formatting | bytes 128 | tf_op jit(solution)/shard_map/all_to_all | solution.py:55
  13.6 0.9 %copy.52 = bf16[1,16,12,128]{3,2,1,0:T(8,128)(2,1)S(1)} copy(f32[1,16,12,128]{3,1,2,0:T(8,128)} %param.11) | data formatting | bytes 147456 | tf_op args[0]
  14.5 0.6 gather_fusion.2
  15.1 0.6 gather_fusion.1
  15.7 0.0 copy-done.2
  15.7 0.2 fusion.4
  15.9 0.0 copy-done.1
  15.9 0.3 fusion.1
  16.2 0.0 all-to-all-done.2
  16.2 3.7 %all-to-all-start = ((s32[8,1,2]{2,1,0:T(1,128)}), s32[8,1,2]{2,1,0:T(1,128)S(1)}, u32[]{:S(2)}, u32[]{:S(2)}) async-start(s32[8,1,2]{2,1,0:T(1,128)} %copy.36), calls=%async_computation | async-start | bytes 8192 | tf_op jit(solution)/shard_map/all_to_all | solution.py:55
  20.0 0.6 copy.43
  20.6 4.0 %all-to-all-done = s32[8,1,2]{2,1,0:T(1,128)S(1)} async-done(((s32[8,1,2]{2,1,0:T(1,128)}), s32[8,1,2]{2,1,0:T(1,128)S(1)}, u32[]{:S(2)}, u32[]{:S(2)}) %all-to-all-start) | async-done | bytes 96 | tf_op jit(solution)/shard_map/all_to_all | solution.py:55
  24.6 5.1 %all-to-all-start.3 = ((f32[4,2,12,128]{3,1,2,0:T(2,128)}), f32[4,2,12,128]{3,1,2,0:T(2,128)S(1)}, u32[]{:S(2)}, u32[]{:S(2)}) async-start(f32[4,2,12,128]{3,1,2,0:T(2,128)} %copy.43), calls=%async_computation.3 | async-start | bytes 98304 | tf_op jit(solution)/shard_map/all_to_all | solution.py:58
  29.7 0.6 gather_fusion
  30.3 0.7 %copy.38 = f32[8,2,12,128]{3,1,2,0:T(2,128)} copy(f32[8,2,12,128]{3,2,1,0:T(8,128)S(1)} %fusion.1) | data formatting | bytes 196608 | tf_op jit(solution)/shard_map/pcmk,pcki->pcmi/dot_general | solution.py:15
  30.9 0.5 broadcast.122
  31.5 0.7 reduce.6
  32.1 0.1 eq.34
  32.2 0.7 reduce.7
  32.9 0.1 eq.30
  33.0 2.4 %all-to-all-done.3 = f32[4,2,12,128]{3,1,2,0:T(2,128)S(1)} async-done(((f32[4,2,12,128]{3,1,2,0:T(2,128)}), f32[4,2,12,128]{3,1,2,0:T(2,128)S(1)}, u32[]{:S(2)}, u32[]{:S(2)}) %all-to-all-start.3) | async-done | bytes 49184 | tf_op jit(solution)/shard_map/all_to_all | solution.py:58
  35.4 3.4 %all-to-all-start.1 = ((f32[8,2,12,128]{3,1,2,0:T(2,128)}), f32[8,2,12,128]{3,1,2,0:T(2,128)S(1)}, u32[]{:S(2)}, u32[]{:S(2)}) async-start(f32[8,2,12,128]{3,1,2,0:T(2,128)} %copy.38), calls=%async_computation.1 | async-start | bytes 196608 | tf_op jit(solution)/shard_map/all_to_all | solution.py:52
  38.8 0.3 fusion.18
  39.1 4.8 %all-to-all-done.1 = f32[8,2,12,128]{3,1,2,0:T(2,128)S(1)} async-done(((f32[8,2,12,128]{3,1,2,0:T(2,128)}), f32[8,2,12,128]{3,1,2,0:T(2,128)S(1)}, u32[]{:S(2)}, u32[]{:S(2)}) %all-to-all-start.1) | async-done | bytes 98336 | tf_op jit(solution)/shard_map/all_to_all | solution.py:52
  43.9 0.2 fusion.14
  44.1 0.0 copy-done
  44.1 0.4 fusion.24
  44.5 11.8 %psum.14 = f32[12]{0:T(128)S(1)} all-reduce(f32[12]{0:T(128)S(1)} %get-tuple-element.8), channel_id=1, replica_groups=mesh['level'=4,'dev'=8] {'dev'}, use_global_device_ids=true, to_apply=%region_1.2 | all-reduce | flops 12 | bytes 96 | tf_op jit(solution)/shard_map/psum | solution.py:72
  56.3 9.8 %psum.15 = f32[12]{0:T(128)S(1)} all-reduce(f32[12]{0:T(128)S(1)} %psum.14), channel_id=1, replica_groups=mesh['level'=4,'dev'=8] {'level'}, use_global_device_ids=true, to_apply=%region_2.3 | all-reduce | flops 12 | bytes 96 | tf_op jit(solution)/shard_map/psum | solution.py:72
  66.0 0.5 broadcast_multiply_fusion
  66.6 0.7 copy.46
  (5 shorter events, 0.1 us)
Async XLA Ops:
  0.6 43.5 %copy-start = (bf16[1,16,128,128]{3,2,1,0:T(8,128)(2,1)S(1)}, bf16[1,16,128,128]{3,2,1,0:T(8,128)(2,1)}, u32[]{:S(2)}) copy-start(bf16[1,16,128,128]{3,2,1,0:T(8,128)(2,1)} %param.13) | copy-start | bytes 1572868
  0.6 0.7 %copy-start.3 = (s32[1,1,4,2]{2,3,1,0:T(2,128)S(1)}, s32[1,1,4,2]{2,3,1,0:T(2,128)}, u32[]{:S(2)}) copy-start(s32[1,1,4,2]{2,3,1,0:T(2,128)} %param.19) | copy-start | bytes 100
  0.7 15.0 %copy-start.2 = (bf16[1,1,4,2,128,128]{5,4,3,2,1,0:T(8,128)(2,1)S(1)}, bf16[1,1,4,2,128,128]{5,4,3,2,1,0:T(8,128)(2,1)}, u32[]{:S(2)}) copy-start(bf16[1,1,4,2,128,128]{5,4,3,2,1,0:T(8,128)(2,1)} %param.21) | copy-start | bytes 786436
  0.7 15.2 %copy-start.1 = (bf16[1,1,8,2,128,128]{5,4,3,2,1,0:T(8,128)(2,1)S(1)}, bf16[1,1,8,2,128,128]{5,4,3,2,1,0:T(8,128)(2,1)}, u32[]{:S(2)}) copy-start(bf16[1,1,8,2,128,128]{5,4,3,2,1,0:T(8,128)(2,1)} %param.17) | copy-start | bytes 1572868
  2.1 14.2 %all-to-all-start.2 = ((s32[4,1,2]{2,1,0:T(1,128)}), s32[4,1,2]{2,1,0:T(1,128)S(1)}, u32[]{:S(2)}, u32[]{:S(2)}) async-start(s32[4,1,2]{2,1,0:T(1,128)} %copy.41), calls=%async_computation.2 | async-start | bytes 4096 | tf_op jit(solution)/shard_map/all_to_all | solution.py:65
  16.2 8.3 %all-to-all-start = ((s32[8,1,2]{2,1,0:T(1,128)}), s32[8,1,2]{2,1,0:T(1,128)S(1)}, u32[]{:S(2)}, u32[]{:S(2)}) async-start(s32[8,1,2]{2,1,0:T(1,128)} %copy.36), calls=%async_computation | async-start | bytes 8192 | tf_op jit(solution)/shard_map/all_to_all | solution.py:55
  24.6 10.8 %all-to-all-start.3 = ((f32[4,2,12,128]{3,1,2,0:T(2,128)}), f32[4,2,12,128]{3,1,2,0:T(2,128)S(1)}, u32[]{:S(2)}, u32[]{:S(2)}) async-start(f32[4,2,12,128]{3,1,2,0:T(2,128)} %copy.43), calls=%async_computation.3 | async-start | bytes 98304 | tf_op jit(solution)/shard_map/all_to_all | solution.py:58
  35.4 8.5 %all-to-all-start.1 = ((f32[8,2,12,128]{3,1,2,0:T(2,128)}), f32[8,2,12,128]{3,1,2,0:T(2,128)S(1)}, u32[]{:S(2)}, u32[]{:S(2)}) async-start(f32[8,2,12,128]{3,1,2,0:T(2,128)} %copy.38), calls=%async_computation.1 | async-start | bytes 196608 | tf_op jit(solution)/shard_map/all_to_all | solution.py:52
